TPU v7x, 256 devices: a whole 4x4x8 slice. The times are simulated.
256 devices in a mesh: batch: 16 (over z, core), vocab: 16 (over y, x).
Axes of the slice: x: 4, y: 4, z: 8, core: 2. Of those that a mesh axis runs over, the one named last changes fastest.
Arguments:
- hidden: bfloat16 [2048, 4096], P('batch'), may hold values from -40 to 40
- exit_layer: int32 [2048], P('batch'), may hold values from 0 to 7
- exit_gains: float32 [8, 4096], replicated, may hold values from 0.1 to 1.9
- unembed: bfloat16 [4096, 128256], P(None, ('batch', 'vocab')), may hold values from -10 to 10
- targets: int32 [2048], replicated, may hold values from 0 to 128255
- values: float32 [2048], P('batch'), may hold values from -6 to 6
- rewards: float32 [2048], P('batch'), may hold values from -2 to 2
- ref_logprob: float32 [2048], P('batch'), may hold values from -16 to -6
- segment_end: int32 [2048], P('batch'), may hold values 0 or 1
Outputs:
- logprob: float32 [2048], P('batch')
- advantages: float32 [2048], P('batch')
All inputs are finite; a program needn't handle non-finite values. No bound on the sum of `segment_end` on one device may be relied on, other than what follows from the above.
Results may differ from a plain program's by a relative error of at most 0.00054.
Values may be sent and summed in bfloat16 or wider, within the bound.
A program may use at most 128 MiB of HBM per device.

v0:
```python
import functools

import jax
import jax.numpy as jnp
from jax import lax
from jax.experimental import pallas as pl
from jax.experimental.pallas import tpu as pltpu
from jax.sharding import Mesh
from jax.sharding import PartitionSpec as P

MESH = pl.DeviceIdType.MESH
F32 = jnp.float32
epsilon_norm = 1e-05
discount = 1.0
trace_decay = 0.999
penalty_weight = 0.1

OFFSETS = (None, 1, -1, 2, -2, 3, -3, 4, 0)
SLOT = {0: 8, 1: 1, -1: 2, 2: 3, -2: 4, 3: 5, -3: 6, 4: 7, -4: 7}
ORDER = (0, 2, 1, 3)


def kernel(
    hidden_hbm, layer_hbm, gains_hbm, w_hbm, targets_hbm, values_hbm, rewards_hbm, ref_hbm, end_hbm,
    out_ref,
    hid, lay, gains, w_own, w_peer, tgt, val, rew, ref, end,
    tok, layc, inv, a12, b12, a56, b56, a7, b7, want, inf, s1, s2, lps,
    load_sem, known_sem, w_sem, z_sem, piece_sem, inf_sem, extra_sem, xy_sem, send_sem, small_recv, small_send,
):
    x, y, z, c = (lax.axis_index(a) for a in ("x", "y", "z", "core"))
    width = hid.shape[1]
    acc12, acc56, acc7 = (a12, b12), (a56, b56), (a7, b7)
    cols = w_own.shape[0]
    xp, xm = lax.rem(x + 1, 4), lax.rem(x + 3, 4)
    yp, ym = lax.rem(y + 1, 4), lax.rem(y + 3, 4)
    zp, zm = lax.rem(z + 1, 8), lax.rem(z + 7, 8)
    b = 2 * z + c
    v = 4 * y + x

    qa = lax.rem(x + 2 * y, 4)
    qb = lax.rem(2 * x + y, 4)
    step = width // 16

    def start_col(t, k=0):
        first = lax.rem(qa + k, 4) * 2 * step if t < 2 else width // 2 + lax.rem(qb + k, 4) * 2 * step
        return pl.multiple_of(first + (t % 2) * step, step)

    def hid_load(k):
        rows = pl.ds(32 * k, 32)
        return pltpu.make_async_copy(hidden_hbm.at[rows, :], hid.at[rows, :], load_sem.at[k])

    for k in range(4):
        hid_load(k).start()
    layer_load = pltpu.make_async_copy(layer_hbm, lay, load_sem.at[8])
    layer_load.start()
    gains_load = pltpu.make_async_copy(gains_hbm, gains, load_sem.at[9])
    gains_load.start()

    barrier = pltpu.get_barrier_semaphore()
    in_plane = [{"x": xp}, {"x": xm}, {"y": yp}, {"y": ym}]
    for where in ({"z": zp}, {"z": zm}, *in_plane, {"core": 1 - c}):
        pl.semaphore_signal(barrier, inc=1, device_id=where, device_id_type=MESH)

    def tell(k):
        for where in in_plane:
            pl.semaphore_signal(known_sem.at[k], inc=1, device_id=where, device_id_type=MESH)

    w_load = pltpu.make_async_copy(w_hbm, w_own, w_sem.at[0])
    w_load.start()
    small = ((targets_hbm, tgt), (values_hbm, val), (rewards_hbm, rew), (ref_hbm, ref), (end_hbm, end))
    loads = [pltpu.make_async_copy(a, o, load_sem.at[10 + i]) for i, (a, o) in enumerate(small)]
    for load in loads:
        load.start()

    row_i = lax.broadcasted_iota(jnp.int32, (128, 128), 0)
    lane_i = lax.broadcasted_iota(jnp.int32, (128, 128), 1)
    eye = row_i == lane_i

    def as_column(line):
        return jnp.sum(jnp.where(eye, jnp.broadcast_to(line, (128, 128)), 0.0), axis=1, keepdims=True)

    with jax.named_scope("loadw"):
        layer_load.wait()
        for k in range(4):
            hid_load(k).wait()
            for r in range(32 * k, 32 * k + 32, 16):
                states = hid[r : r + 16, :].astype(F32)
                mean = jnp.mean(states * states, axis=1, keepdims=True)
                inv[r : r + 16, :] = jnp.broadcast_to(lax.rsqrt(mean + epsilon_norm), (16, 128))
        gains_load.wait()
    layc[...] = jnp.broadcast_to(as_column(lay[...].astype(F32)), (128, 128))

    def normalize(col):
        for half in range(step // 128):
            at = pl.ds(pl.multiple_of(col + 128 * half, 128), 128)
            which = layc[...]
            scaling = jnp.broadcast_to(gains[0:1, at], (128, 128))
            for e in range(1, 8):
                scaling = jnp.where(which == float(e), gains[e : e + 1, at], scaling)
            tok[896:1024, at] = (hid[:, at].astype(F32) * inv[...] * scaling).astype(jnp.bfloat16)

    def tile(slot, t, piece=None, k=0):
        row = (slot - 1) * 128
        rows = pl.ds(row, 128) if piece is None else pl.ds(row + 32 * piece, 32)
        return tok.at[rows, pl.ds(start_col(t, k), step)]

    def send(src, dst, recv, where):
        pltpu.make_async_remote_copy(
            src_ref=src, dst_ref=dst, send_sem=send_sem.at[0], recv_sem=recv, device_id=where, device_id_type=MESH
        ).start()

    def arrived(slot, t, piece):
        return z_sem.at[slot, t] if piece is None else piece_sem.at[slot, 4 * t + piece]

    def send_z(src_slot, t, up, piece=None):
        dst_slot = SLOT[OFFSETS[src_slot] + (-1 if up else 1)]
        send(tile(src_slot, t, piece), tile(dst_slot, t, piece), arrived(dst_slot, t, piece), {"z": zp if up else zm})

    def send_xy(slot, t, piece=None):
        targets = [{"x": xp}, {"x": xm}] if t < 2 else [{"y": yp}, {"y": ym}]
        if slot > 2:
            targets.append((({"y": yp}, {"y": ym}) if t < 2 else ({"x": xp}, {"x": xm}))[t % 2])
        for where in targets:
            send(tile(slot, t, piece), tile(slot, t, piece), xy_sem.at[slot, t], where)

    def send_extra(half):
        for t in (half, half + 2):
            send(tile(8, t, k=2), tile(2, t, k=2), extra_sem.at[1, t], {"z": zp})
            send(tile(8, t, k=2), tile(1, t, k=2), extra_sem.at[0, t], {"z": zm})

    def wait_z(slot, t, piece=None):
        there = tile(slot, t, piece)
        pltpu.make_async_copy(there, there, arrived(slot, t, piece)).wait()

    FIRST = [(t, piece) for half in (0, 1) for piece in range(4) for t in (half, half + 2)]
    with jax.named_scope("norm2"):
        normalize(start_col(0))
        normalize(start_col(2))
    with jax.named_scope("barrier"):
        pl.semaphore_wait(barrier, 7)
    for t, piece in FIRST[:8]:
        send_z(8, t, True, piece)
        send_z(8, t, False, piece)
    normalize(start_col(1))
    normalize(start_col(3))
    for t, piece in FIRST[8:]:
        send_z(8, t, True, piece)
        send_z(8, t, False, piece)

    def swap(k):
        part = pl.ds(k * (width // 8), width // 8)
        pltpu.make_async_remote_copy(
            src_ref=w_hbm.at[:, part], dst_ref=w_peer.at[:, part], send_sem=w_sem.at[1], recv_sem=w_sem.at[2],
            device_id={"core": 1 - c}, device_id_type=MESH,
        ).start()

    swap(0)
    swap(1)
    for load in loads:
        load.wait()

    sub = lax.broadcasted_iota(jnp.int32, (8, 128), 0)
    lanes = lax.broadcasted_iota(jnp.int32, (8, 128), 1)

    def packed(first, second, third):
        return jnp.where(sub == 0, first, jnp.where(sub == 1, second, jnp.where(sub == 2, third, 0.0)))

    def inf_at(core, j):
        return pl.ds(pl.multiple_of(core * 64 + 8 * j, 8), 8)

    inf[inf_at(c, 0), :] = packed(
        val[...], rew[...] + penalty_weight * ref[...] - val[...], 1.0 - end[...].astype(F32)
    )
    def inf_tile(slot):
        return inf.at[inf_at(c, OFFSETS[slot] % 8), :]

    def send_inf(src_slot, up):
        slot = SLOT[OFFSETS[src_slot] + (-1 if up else 1)]
        pltpu.make_async_remote_copy(
            src_ref=inf_tile(src_slot), dst_ref=inf_tile(slot), send_sem=small_send.at[0], recv_sem=inf_sem.at[slot],
            device_id={"z": zp if up else zm}, device_id_type=MESH,
        ).start()

    def wait_inf(slot):
        pltpu.make_async_copy(inf_tile(slot), inf_tile(slot), inf_sem.at[slot]).wait()

    send_inf(8, True)
    send_inf(8, False)

    def rest(k, _):
        for t in range(4):
            normalize(start_col(t, k))
        return 0

    with jax.named_scope("rest"):
        lax.fori_loop(1, 4, rest, 0)

    for slot in range(1, 9):
        line = tgt[pl.ds(2 * lax.rem(z + OFFSETS[slot] + 8, 8) + c, 1), :]
        want[:, (slot - 1) * 128 : (slot - 1) * 128 + 128] = line

    own_start = (b * 16 + v) * cols
    peer_start = ((2 * z + 1 - c) * 16 + v) * cols
    contract = (((1,), (1,)), ((), ()))

    def score(slots, now=True):
        at = pl.ds((slots[0] - 1) * 128, 128 * len(slots))
        own = lax.dot_general(w_own[...], tok[at, :], contract, preferred_element_type=F32)
        peer = lax.dot_general(w_peer[...], tok[at, :], contract, preferred_element_type=F32)
        reduce(slots, own, peer, now)

    def mac(slots, sums, t, k, tiles=2, start=False):
        at = pl.ds((slots[0] - 1) * 128, 128 * len(slots))
        depth = pl.ds(start_col(t, k), tiles * step)
        for weights, total in zip((w_own, w_peer), sums):
            part = lax.dot_general(weights[:, depth], tok[at, depth], contract, preferred_element_type=F32)
            total[...] = part if start else total[...] + part

    def reduce(slots, own, peer, now=True):
        slot, count = slots[0], 128 * len(slots)
        top = jnp.maximum(jnp.max(own, axis=0, keepdims=True), jnp.max(peer, axis=0, keepdims=True))
        total = jnp.sum(jnp.exp(own - top), axis=0, keepdims=True) + jnp.sum(jnp.exp(peer - top), axis=0, keepdims=True)
        wanted = want[:, (slot - 1) * 128 : (slot - 1) * 128 + count]
        columns = lax.broadcasted_iota(jnp.int32, (cols, count), 0)
        pick = jnp.sum(jnp.where(columns == wanted - own_start, own, 0.0), axis=0, keepdims=True) + jnp.sum(
            jnp.where(columns == wanted - peer_start, peer, 0.0), axis=0, keepdims=True
        )
        for k, slot in enumerate(slots):
            cut = slice(128 * k, 128 * k + 128)
            j = OFFSETS[slot] % 8
            s1[0, 8 * j : 8 * j + 8, :] = packed(top[:, cut], total[:, cut], pick[:, cut])
        for slot in slots if now else ():
            send_part(slot)

    def send_part(slot):
            j = OFFSETS[slot] % 8
            for d in range(1, 8):
                pltpu.make_async_remote_copy(
                    src_ref=s1.at[0, pl.ds(8 * j, 8), :], dst_ref=s1.at[8 - d, pl.ds(8 * ((j - d) % 8), 8), :],
                    send_sem=small_send.at[1], recv_sem=small_recv.at[1],
                    device_id={"z": lax.rem(z + d, 8)}, device_id_type=MESH,
                ).start()

    def wait_xy(slot, t):
        tiles = tok.at[pl.ds(0, 128), pl.ds(0, step * (3 if slot > 2 else 2))]
        pltpu.make_async_copy(tiles, tiles, xy_sem.at[slot, t]).wait()

    def arrivals(phase, between=()):
        up_slot, down_slot = (SLOT[-phase], SLOT[phase])
        for n, (t, piece) in enumerate(FIRST if phase < 3 else [(t, None) for t in ORDER]):
            if phase < 4:
                onward = phase == 1 or piece in (None, 3)
                through = piece if phase == 1 else None
                wait_z(up_slot, t, piece)
                if onward and (phase < 3 or t % 2 == 0):
                    send_z(up_slot, t, True, through)
                send_xy(up_slot, t, piece)
                wait_z(down_slot, t, piece)
                if onward and (phase < 3 or t % 2 == 1):
                    send_z(down_slot, t, False, through)
                send_xy(down_slot, t, piece)
                for work in between[2 * n : 2 * n + 2]:
                    mac(*work)
                if phase == 1 and 4 <= n < 16 and n % 2 == 0:
                    swap(n // 2)
            else:
                wait_z(7, t)
                send_xy(7, t)

        if phase < 4:
            wait_inf(up_slot)
            send_inf(up_slot, True)
            wait_inf(down_slot)
            if phase < 3:
                send_inf(down_slot, False)
        else:
            wait_inf(7)

    def wait_extra(slot, t):
        there = tile(slot, t, k=2)
        pltpu.make_async_copy(there, there, extra_sem.at[slot - 1, t]).wait()

    tell(0)
    with jax.named_scope("arrive1"):
        arrivals(1)
    with jax.named_scope("arrive2"):
        arrivals(2)
    send_extra(0)
    pl.semaphore_wait(known_sem.at[0], 4)
    tell(1)
    with jax.named_scope("wload"):
        w_load.wait()
        pltpu.make_async_copy(w_peer, w_peer, w_sem.at[2]).wait()
    with jax.named_scope("score8"):
        score((8,), False)
    with jax.named_scope("waitxy12"):
        for t in range(4):
            wait_xy(1, t)
            wait_xy(2, t)
    with jax.named_scope("arrive3"):
        arrivals(3, [((1, 2), acc12, t, k, 2, t + k == 0) for k in (0, 1, 3) for t in (0, 2)])
    send_extra(1)
    with jax.named_scope("mac56n"):
        mac((5, 6), acc56, 0, 0, start=True)
        mac((5, 6), acc56, 2, 0)
    with jax.named_scope("waitxy34"):
        for t in range(4):
            wait_xy(3, t)
            wait_xy(4, t)
    with jax.named_scope("score34"):
        score((3, 4), False)

    def arrived_mac(slots, sums, t):
        with jax.named_scope(f"wait{slots[0]}{t}"):
            for slot in slots:
                wait_xy(slot, t)
        with jax.named_scope(f"mac{slots[0]}{t}"):
            for k in (1, 2, 3):
                mac(slots, sums, t, k, 1)

    def extra_mac(t):
        with jax.named_scope(f"waitex{t}"):
            wait_extra(1, t)
            wait_extra(2, t)
        mac((1, 2), acc12, t, 2, 1)

    arrived_mac((5, 6), acc56, 0)
    extra_mac(0)
    extra_mac(2)
    pl.semaphore_wait(known_sem.at[1], 4)
    tell(2)
    with jax.named_scope("arrive4"):
        arrivals(4)
    for slot in (8, 3, 4):
        send_part(slot)
    own_inf = inf.at[pl.ds(pl.multiple_of(64 * c, 8), 64), :]
    inf_send = pltpu.make_async_remote_copy(
        src_ref=own_inf, dst_ref=own_inf, send_sem=small_send.at[4], recv_sem=small_recv.at[4],
        device_id={"core": 1 - c}, device_id_type=MESH,
    )
    inf_send.start()
    with jax.named_scope("mac7n"):
        mac((7,), acc7, 0, 0, start=True)
        mac((7,), acc7, 2, 0)

    arrived_mac((5, 6), acc56, 2)
    with jax.named_scope("pre"):
        inf_send.wait()
        known = []
        vals = [inf[pl.ds(64 * core, 8, stride=8), :] for core in range(2)]
        after = [vals[1], jnp.where(sub + z == 7, 0.0, pltpu.roll(vals[0], 7, 0))]
        steps = (1, 2, 4, 8, 16, 32, 64)
        for core in range(2):
            base = inf[pl.ds(64 * core + 1, 8, stride=8), :]
            keeping = inf[pl.ds(64 * core + 2, 8, stride=8), :]
            following = jnp.where(lanes < 127, pltpu.roll(vals[core], 127, 1), pltpu.roll(after[core], 127, 1))
            factor = discount * trace_decay * keeping
            factors = []
            for k in steps:
                factors.append(factor)
                factor = factor * jnp.where(lanes < 128 - k, pltpu.roll(factor, 128 - k, 1), 1.0)
            known.append((base + discount * following * keeping, factors, factor))

    extra_mac(1)
    extra_mac(3)
    with jax.named_scope("reduce12"):
        reduce((1, 2), acc12[0][...], acc12[1][...])
    arrived_mac((5, 6), acc56, 1)
    arrived_mac((5, 6), acc56, 3)
    with jax.named_scope("reduce56"):
        reduce((5, 6), acc56[0][...], acc56[1][...])
    pl.semaphore_wait(known_sem.at[2], 4)
    arrived_mac((7,), acc7, 0)
    arrived_mac((7,), acc7, 2)
    arrived_mac((7,), acc7, 1)
    arrived_mac((7,), acc7, 3)
    with jax.named_scope("score7"):
        reduce((7,), acc7[0][...], acc7[1][...])

    with jax.named_scope("s1"):
        seven = s1.at[pl.ds(1, 7)]
        pltpu.make_async_copy(seven, seven, small_recv.at[1]).wait()

    def joined(tops):
        top = functools.reduce(jnp.maximum, tops)
        return top, [jnp.exp(t - top) for t in tops]

    top, shares = joined([s1[k, pl.ds(0, 8, stride=8), :] for k in range(8)])
    total = sum(s1[k, pl.ds(1, 8, stride=8), :] * shares[k] for k in range(8))
    s2[v, 0] = top + jnp.log(total)
    s2[v, 1] = sum(s1[k, pl.ds(2, 8, stride=8), :] for k in range(8))
    for k in range(1, 16):
        pltpu.make_async_remote_copy(
            src_ref=s2.at[v], dst_ref=s2.at[v], send_sem=small_send.at[2], recv_sem=small_recv.at[2],
            device_id={"y": lax.rem(y + k // 4, 4), "x": lax.rem(x + k % 4, 4)}, device_id_type=MESH,
        ).start()
    fifteen = s2.at[pl.ds(0, 15)]
    with jax.named_scope("s2"):
        pltpu.make_async_copy(fifteen, fifteen, small_recv.at[2]).wait()
    top, shares = joined([s2[k, 0] for k in range(16)])
    lps[c] = sum(s2[k, 1] for k in range(16)) - (top + jnp.log(sum(shares)))
    lp_send = pltpu.make_async_remote_copy(
        src_ref=lps.at[c], dst_ref=lps.at[c], send_sem=small_send.at[3], recv_sem=small_recv.at[3],
        device_id={"core": 1 - c}, device_id_type=MESH,
    )
    lp_send.start()
    with jax.named_scope("s3"):
        lp_send.wait()

    local = []
    for core in range(2):
        base, factors, _ = known[core]
        line = base - penalty_weight * lps[core]
        for k, f in zip(steps, factors):
            line = line + f * jnp.where(lanes < 128 - k, pltpu.roll(line, 128 - k, 1), 0.0)
        local.append(line)

    def spread(column):
        return jnp.broadcast_to(column, (8, 128))

    head = [spread(line[:, 0:1]) for line in local]
    prod = [spread(known[core][2][:, 0:1]) for core in range(2)]
    in_range = sub + z < 8
    tail = jnp.where(in_range, head[0] + prod[0] * head[1], 0.0)
    reach = jnp.where(in_range, prod[0] * prod[1], 0.0)
    for k in (1, 2, 4):
        tail = tail + reach * jnp.where(sub < 8 - k, pltpu.roll(tail, 8 - k, 0), 0.0)
        reach = reach * jnp.where(sub < 8 - k, pltpu.roll(reach, 8 - k, 0), 0.0)
    beyond = pltpu.roll(jnp.where(sub == 0, 0.0, tail), 7, 0)
    first = c == 0
    incoming = jnp.where(first, head[1] + prod[1] * beyond, beyond)
    mine = jnp.where(first, local[0], local[1]) + jnp.where(first, known[0][2], known[1][2]) * incoming
    out_ref[...] = jnp.where(sub == 0, lps[c], jnp.where(sub == 1, pltpu.roll(mine, 1, 0), 0.0))

    with jax.named_scope("endsend"):
        seven_blocks = tok.at[pl.ds(0, 896), :]
        pltpu.make_async_copy(seven_blocks, seven_blocks, send_sem.at[0]).wait()
        pltpu.make_async_copy(w_peer, w_peer, w_sem.at[1]).wait()
        others = inf.at[pl.ds(0, 56), :]
        pltpu.make_async_copy(others, others, small_send.at[0]).wait()
        pltpu.make_async_copy(seven, seven, small_send.at[1]).wait()
        pltpu.make_async_copy(fifteen, fifteen, small_send.at[2]).wait()


def per_device(hidden, exit_layer, exit_gains, unembed, targets, values, rewards, ref_logprob, segment_end):
    width, cols = unembed.shape
    line = lambda a: a.reshape(1, 128)
    anywhere = pl.BlockSpec(memory_space=pl.ANY)
    vmem = pl.BlockSpec(memory_space=pltpu.VMEM)
    i32 = jnp.int32
    both = pl.pallas_call(
        kernel,
        out_shape=jax.ShapeDtypeStruct((8, 128), F32),
        in_specs=[anywhere] * 9,
        out_specs=vmem,
        scratch_shapes=[
            pltpu.VMEM((128, width), jnp.bfloat16),
            pltpu.VMEM((1, 128), i32),
            pltpu.VMEM((8, width), F32),
            pltpu.VMEM((cols, width), jnp.bfloat16),
            pltpu.VMEM((cols, width), jnp.bfloat16),
            pltpu.VMEM((16, 128), i32),
            pltpu.VMEM((1, 128), F32),
            pltpu.VMEM((1, 128), F32),
            pltpu.VMEM((1, 128), F32),
            pltpu.VMEM((1, 128), i32),
            pltpu.VMEM((1024, width), jnp.bfloat16),
            pltpu.VMEM((128, 128), F32),
            pltpu.VMEM((128, 128), F32),
            pltpu.VMEM((cols, 256), F32),
            pltpu.VMEM((cols, 256), F32),
            pltpu.VMEM((cols, 256), F32),
            pltpu.VMEM((cols, 256), F32),
            pltpu.VMEM((cols, 128), F32),
            pltpu.VMEM((cols, 128), F32),
            pltpu.VMEM((1, 1024), i32),
            pltpu.VMEM((128, 128), F32),
            pltpu.VMEM((8, 64, 128), F32),
            pltpu.VMEM((16, 2, 8, 128), F32),
            pltpu.VMEM((2, 8, 128), F32),
            pltpu.SemaphoreType.DMA((15,)),
            pltpu.SemaphoreType.REGULAR((3,)),
            pltpu.SemaphoreType.DMA((3,)),
            pltpu.SemaphoreType.DMA((8, 4)),
            pltpu.SemaphoreType.DMA((5, 16)),
            pltpu.SemaphoreType.DMA((8,)),
            pltpu.SemaphoreType.DMA((2, 4)),
            pltpu.SemaphoreType.DMA((8, 4)),
            pltpu.SemaphoreType.DMA((1,)),
            pltpu.SemaphoreType.DMA((5,)),
            pltpu.SemaphoreType.DMA((5,)),
        ],
        compiler_params=pltpu.CompilerParams(
            collective_id=0, has_side_effects=True, vmem_limit_bytes=60 * 1024 * 1024
        ),
    )(
        hidden, line(exit_layer), exit_gains, unembed.T, targets.reshape(16, 128),
        line(values), line(rewards), line(ref_logprob), line(segment_end),
    )
    return both[0], both[1]


def solution(mesh):
    torus = Mesh(mesh.devices.reshape(8, 2, 4, 4), ("z", "core", "y", "x"))
    tokens = P(("z", "core"))
    return jax.shard_map(
        per_device,
        mesh=torus,
        in_specs=(
            P(("z", "core"), None), tokens, P(), P(None, ("z", "core", "y", "x")), P(), tokens, tokens, tokens, tokens,
        ),
        out_specs=(tokens, tokens),
        check_vma=False,
    )
```

profile of v0, /device:TPU:1, one launch (start us, length us, event | category | flops | bytes accessed | tf_op | source)
XLA Modules:
  0.0 58.7 jit_solution(16334773130240962881)
XLA Ops:
  0.6 56.8 %shard_map.104 = f32[8,128]{1,0:T(8,128)} custom-call(bf16[128,4096]{1,0:T(8,128)(2,1)} %hidden_hbm.1, s32[1,128]{1,0:T(1,128)} %bitcast.13, f32[8,4096]{1,0:T(8,128)} %gains_hbm.1, bf16[501,4096]{1,0:T(8,128)(2,1)} %bitcast.11, s32[16,128]{1,0:T(8,128)} %bitcast.12, f32[1,128]{1,0:T(1,128)} %bitcast.14, f32[1,128]{1,0:T(1,128)} %bitcast.15, ...), custom_call_target="tpu_custom_call" | custom-call | tf_op jit(solution)/shard_map/pallas_call | solution.py:451
  57.4 1.3 %slice_bitcast_fusion = (f32[128]{0:T(128)}, f32[128]{0:T(128)}) fusion(f32[8,128]{1,0:T(8,128)} %shard_map.104), kind=kLoop, calls=%fused_computation | loop fusion | bytes 2048 | tf_op jit(solution)/shard_map/squeeze | solution.py:500
where the time goes:
time: 58.8 us; the launch traced here: 58.7 us
  Pallas kernels  56.8 us (97%)
  local copies, waits for them, and re-layouts  1.26 us (2%)
  between operations  0.64 us (1%)
    pallas_call x1, Pallas kernels, per_device(): pl.pallas_call(kernel, out_shape=jax.ShapeDtypeStruct((8, 128), F32), in_...  56.8 us
    squeeze x1, local copies, waits for them, and re-layouts, per_device(): return (both[0], both[1])  1.26 us

commit v1 on v0

--- a/solution.py
+++ b/solution.py
@@ -25,7 +25,7 @@
     out_ref,
     hid, lay, gains, w_own, w_peer, tgt, val, rew, ref, end,
     tok, layc, inv, a12, b12, a56, b56, a7, b7, want, inf, s1, s2, lps,
-    load_sem, known_sem, w_sem, z_sem, piece_sem, inf_sem, extra_sem, xy_sem, send_sem, small_recv, small_send,
+    load_sem, known_sem, w_sem, z_sem, piece_sem, inf_sem, s1_recv, extra_sem, xy_sem, send_sem, small_recv, small_send,
 ):
     x, y, z, c = (lax.axis_index(a) for a in ("x", "y", "z", "core"))
     width = hid.shape[1]
@@ -228,18 +228,25 @@
         for k, slot in enumerate(slots):
             cut = slice(128 * k, 128 * k + 128)
             j = OFFSETS[slot] % 8
-            s1[0, 8 * j : 8 * j + 8, :] = packed(top[:, cut], total[:, cut], pick[:, cut])
+            s1[c, 0, 8 * j : 8 * j + 8, :] = packed(top[:, cut], total[:, cut], pick[:, cut])
         for slot in slots if now else ():
             send_part(slot)
 
+    def part_copy(slot, d):
+        j = OFFSETS[slot] % 8
+        return pltpu.make_async_remote_copy(
+            src_ref=s1.at[c, 0, pl.ds(8 * j, 8), :], dst_ref=s1.at[c, (8 - d) % 8, pl.ds(8 * ((j - d) % 8), 8), :],
+            send_sem=small_send.at[1], recv_sem=s1_recv.at[c],
+            device_id={"z": lax.rem(z + d, 8), "core": 1}, device_id_type=MESH,
+        )
+
     def send_part(slot):
-            j = OFFSETS[slot] % 8
-            for d in range(1, 8):
-                pltpu.make_async_remote_copy(
-                    src_ref=s1.at[0, pl.ds(8 * j, 8), :], dst_ref=s1.at[8 - d, pl.ds(8 * ((j - d) % 8), 8), :],
-                    send_sem=small_send.at[1], recv_sem=small_recv.at[1],
-                    device_id={"z": lax.rem(z + d, 8)}, device_id_type=MESH,
-                ).start()
+        for d in (4, 3, 5, 2, 6, 1, 7):
+            part_copy(slot, d).start()
+
+        @pl.when(c == 0)
+        def _():
+            part_copy(slot, 0).start()
 
     def wait_xy(slot, t):
         tiles = tok.at[pl.ds(0, 128), pl.ds(0, step * (3 if slot > 2 else 2))]
@@ -377,35 +384,45 @@
     with jax.named_scope("score7"):
         reduce((7,), acc7[0][...], acc7[1][...])
 
-    with jax.named_scope("s1"):
-        seven = s1.at[pl.ds(1, 7)]
-        pltpu.make_async_copy(seven, seven, small_recv.at[1]).wait()
-
     def joined(tops):
         top = functools.reduce(jnp.maximum, tops)
         return top, [jnp.exp(t - top) for t in tops]
 
-    top, shares = joined([s1[k, pl.ds(0, 8, stride=8), :] for k in range(8)])
-    total = sum(s1[k, pl.ds(1, 8, stride=8), :] * shares[k] for k in range(8))
-    s2[v, 0] = top + jnp.log(total)
-    s2[v, 1] = sum(s1[k, pl.ds(2, 8, stride=8), :] for k in range(8))
-    for k in range(1, 16):
-        pltpu.make_async_remote_copy(
-            src_ref=s2.at[v], dst_ref=s2.at[v], send_sem=small_send.at[2], recv_sem=small_recv.at[2],
-            device_id={"y": lax.rem(y + k // 4, 4), "x": lax.rem(x + k % 4, 4)}, device_id_type=MESH,
-        ).start()
+    def lps_copy():
+        return pltpu.make_async_remote_copy(
+            src_ref=lps, dst_ref=lps, send_sem=small_send.at[3], recv_sem=small_recv.at[3],
+            device_id={"core": 0}, device_id_type=MESH,
+        )
+
     fifteen = s2.at[pl.ds(0, 15)]
-    with jax.named_scope("s2"):
-        pltpu.make_async_copy(fifteen, fifteen, small_recv.at[2]).wait()
-    top, shares = joined([s2[k, 0] for k in range(16)])
-    lps[c] = sum(s2[k, 1] for k in range(16)) - (top + jnp.log(sum(shares)))
-    lp_send = pltpu.make_async_remote_copy(
-        src_ref=lps.at[c], dst_ref=lps.at[c], send_sem=small_send.at[3], recv_sem=small_recv.at[3],
-        device_id={"core": 1 - c}, device_id_type=MESH,
-    )
-    lp_send.start()
-    with jax.named_scope("s3"):
-        lp_send.wait()
+    eight, seven = s1.at[0], s1.at[1, pl.ds(1, 7)]
+
+    @pl.when(c == 1)
+    def _():
+        with jax.named_scope("s1"):
+            pltpu.make_async_copy(seven, seven, s1_recv.at[1]).wait()
+            pltpu.make_async_copy(eight, eight, s1_recv.at[0]).wait()
+        for core in range(2):
+            top, shares = joined([s1[core, k, pl.ds(0, 8, stride=8), :] for k in range(8)])
+            total = sum(s1[core, k, pl.ds(1, 8, stride=8), :] * shares[k] for k in range(8))
+            s2[v, 2 * core] = top + jnp.log(total)
+            s2[v, 2 * core + 1] = sum(s1[core, k, pl.ds(2, 8, stride=8), :] for k in range(8))
+        for k in (10, 6, 9, 11, 14, 2, 8, 5, 7, 13, 15, 1, 3, 4, 12):
+            pltpu.make_async_remote_copy(
+                src_ref=s2.at[v], dst_ref=s2.at[v], send_sem=small_send.at[2], recv_sem=small_recv.at[2],
+                device_id={"y": lax.rem(y + k // 4, 4), "x": lax.rem(x + k % 4, 4)}, device_id_type=MESH,
+            ).start()
+        with jax.named_scope("s2"):
+            pltpu.make_async_copy(fifteen, fifteen, small_recv.at[2]).wait()
+        for core in range(2):
+            top, shares = joined([s2[k, 2 * core] for k in range(16)])
+            lps[core] = sum(s2[k, 2 * core + 1] for k in range(16)) - (top + jnp.log(sum(shares)))
+        lps_copy().start()
+
+    @pl.when(c == 0)
+    def _():
+        with jax.named_scope("s3"):
+            lps_copy().wait_recv()
 
     local = []
     for core in range(2):
@@ -438,8 +455,16 @@
         pltpu.make_async_copy(w_peer, w_peer, w_sem.at[1]).wait()
         others = inf.at[pl.ds(0, 56), :]
         pltpu.make_async_copy(others, others, small_send.at[0]).wait()
-        pltpu.make_async_copy(seven, seven, small_send.at[1]).wait()
-        pltpu.make_async_copy(fifteen, fifteen, small_send.at[2]).wait()
+
+        @pl.when(c == 0)
+        def _():
+            pltpu.make_async_copy(eight, eight, small_send.at[1]).wait()
+
+        @pl.when(c == 1)
+        def _():
+            pltpu.make_async_copy(seven, seven, small_send.at[1]).wait()
+            pltpu.make_async_copy(fifteen, fifteen, small_send.at[2]).wait()
+            lps_copy().wait_send()
 
 
 def per_device(hidden, exit_layer, exit_gains, unembed, targets, values, rewards, ref_logprob, segment_end):
@@ -475,8 +500,8 @@
             pltpu.VMEM((cols, 128), F32),
             pltpu.VMEM((1, 1024), i32),
             pltpu.VMEM((128, 128), F32),
-            pltpu.VMEM((8, 64, 128), F32),
-            pltpu.VMEM((16, 2, 8, 128), F32),
+            pltpu.VMEM((2, 8, 64, 128), F32),
+            pltpu.VMEM((16, 4, 8, 128), F32),
             pltpu.VMEM((2, 8, 128), F32),
             pltpu.SemaphoreType.DMA((15,)),
             pltpu.SemaphoreType.REGULAR((3,)),
@@ -484,6 +509,7 @@
             pltpu.SemaphoreType.DMA((8, 4)),
             pltpu.SemaphoreType.DMA((5, 16)),
             pltpu.SemaphoreType.DMA((8,)),
+            pltpu.SemaphoreType.DMA((2,)),
             pltpu.SemaphoreType.DMA((2, 4)),
             pltpu.SemaphoreType.DMA((8, 4)),
             pltpu.SemaphoreType.DMA((1,)),

time: 58.8 us -> 56.8 us (0.966)
  Pallas kernels: 56.8 us -> 54.7 us
    pallas_call x1, Pallas kernels: 56.8 us -> 54.7 us  [per_device(): pl.pallas_call(kernel, out_shape=jax.ShapeDtypeStruct((8, 128), F32), in_...]
where the time goes in v1:
time: 56.8 us; the launch traced here: 56.6 us
  Pallas kernels  54.7 us (96%)
  local copies, waits for them, and re-layouts  1.26 us (2%)
  between operations  0.64 us (1%)
    pallas_call x1, Pallas kernels, per_device(): pl.pallas_call(kernel, out_shape=jax.ShapeDtypeStruct((8, 128), F32), in_...  54.7 us
    squeeze x1, local copies, waits for them, and re-layouts, per_device(): return (both[0], both[1])  1.26 us

profile of v1, /device:TPU:1, one launch (start us, length us, event | category | flops | bytes accessed | tf_op | source)
XLA Modules:
  0.0 56.6 jit_solution(16854662994441533130)
XLA Ops:
  0.6 54.7 %shard_map.104 = f32[8,128]{1,0:T(8,128)} custom-call(bf16[128,4096]{1,0:T(8,128)(2,1)} %hidden_hbm.1, s32[1,128]{1,0:T(1,128)} %bitcast.13, f32[8,4096]{1,0:T(8,128)} %gains_hbm.1, bf16[501,4096]{1,0:T(8,128)(2,1)} %bitcast.11, s32[16,128]{1,0:T(8,128)} %bitcast.12, f32[1,128]{1,0:T(1,128)} %bitcast.14, f32[1,128]{1,0:T(1,128)} %bitcast.15, ...), custom_call_target="tpu_custom_call" | custom-call | tf_op jit(solution)/shard_map/pallas_call | solution.py:476
  55.4 1.3 %slice_bitcast_fusion = (f32[128]{0:T(128)}, f32[128]{0:T(128)}) fusion(f32[8,128]{1,0:T(8,128)} %shard_map.104), kind=kLoop, calls=%fused_computation | loop fusion | bytes 2048 | tf_op jit(solution)/shard_map/squeeze | solution.py:526

commit v2 on v1

--- a/solution.py
+++ b/solution.py
@@ -351,6 +351,22 @@
         mac((7,), acc7, 2, 0)
 
     arrived_mac((5, 6), acc56, 2)
+    arrived_mac((5, 6), acc56, 1)
+    arrived_mac((5, 6), acc56, 3)
+    with jax.named_scope("reduce56"):
+        reduce((5, 6), acc56[0][...], acc56[1][...])
+    extra_mac(1)
+    extra_mac(3)
+    with jax.named_scope("reduce12"):
+        reduce((1, 2), acc12[0][...], acc12[1][...])
+    pl.semaphore_wait(known_sem.at[2], 4)
+    arrived_mac((7,), acc7, 0)
+    arrived_mac((7,), acc7, 2)
+    arrived_mac((7,), acc7, 1)
+    arrived_mac((7,), acc7, 3)
+    with jax.named_scope("score7"):
+        reduce((7,), acc7[0][...], acc7[1][...])
+
     with jax.named_scope("pre"):
         inf_send.wait()
         known = []
@@ -368,21 +384,6 @@
                 factor = factor * jnp.where(lanes < 128 - k, pltpu.roll(factor, 128 - k, 1), 1.0)
             known.append((base + discount * following * keeping, factors, factor))
 
-    extra_mac(1)
-    extra_mac(3)
-    with jax.named_scope("reduce12"):
-        reduce((1, 2), acc12[0][...], acc12[1][...])
-    arrived_mac((5, 6), acc56, 1)
-    arrived_mac((5, 6), acc56, 3)
-    with jax.named_scope("reduce56"):
-        reduce((5, 6), acc56[0][...], acc56[1][...])
-    pl.semaphore_wait(known_sem.at[2], 4)
-    arrived_mac((7,), acc7, 0)
-    arrived_mac((7,), acc7, 2)
-    arrived_mac((7,), acc7, 1)
-    arrived_mac((7,), acc7, 3)
-    with jax.named_scope("score7"):
-        reduce((7,), acc7[0][...], acc7[1][...])
 
     def joined(tops):
         top = functools.reduce(jnp.maximum, tops)

time: 56.8 us -> 57.1 us (level)
  no operation moved by 1% of the time
where the time goes in v2:
time: 57.1 us; the launch traced here: 56.9 us
  Pallas kernels  55 us (96%)
  local copies, waits for them, and re-layouts  1.26 us (2%)
  between operations  0.64 us (1%)
    pallas_call x1, Pallas kernels, per_device(): pl.pallas_call(kernel, out_shape=jax.ShapeDtypeStruct((8, 128), F32), in_...  55 us
    squeeze x1, local copies, waits for them, and re-layouts, per_device(): return (both[0], both[1])  1.26 us

profile of v2, /device:TPU:1, one launch (start us, length us, event | category | flops | bytes accessed | tf_op | source)
XLA Modules:
  0.0 56.9 jit_solution(7573900754829485099)
XLA Ops:
  0.6 55.0 %shard_map.104 = f32[8,128]{1,0:T(8,128)} custom-call(bf16[128,4096]{1,0:T(8,128)(2,1)} %hidden_hbm.1, s32[1,128]{1,0:T(1,128)} %bitcast.13, f32[8,4096]{1,0:T(8,128)} %gains_hbm.1, bf16[501,4096]{1,0:T(8,128)(2,1)} %bitcast.11, s32[16,128]{1,0:T(8,128)} %bitcast.12, f32[1,128]{1,0:T(1,128)} %bitcast.14, f32[1,128]{1,0:T(1,128)} %bitcast.15, ...), custom_call_target="tpu_custom_call" | custom-call | tf_op jit(solution)/shard_map/pallas_call | solution.py:477
  55.7 1.3 %slice_bitcast_fusion = (f32[128]{0:T(128)}, f32[128]{0:T(128)}) fusion(f32[8,128]{1,0:T(8,128)} %shard_map.104), kind=kLoop, calls=%fused_computation | loop fusion | bytes 2048 | tf_op jit(solution)/shard_map/squeeze | solution.py:527
